TPU v7x, 64 devices: a 2x2x8 block of a 4x4x8 slice. The times are simulated.
64 devices in a mesh: dp: 4 (over x, y), ep: 16 (over z, core).
Axes of the slice: x: 2, y: 2, z: 8, core: 2. Of those that a mesh axis runs over, the one named last changes fastest.
The devices are a block of a 4x4x8 slice.
Arguments:
- x_disp: bfloat16 [64, 32, 96, 1024], P('dp', 'ep'), parts along dimension 0
- w_gate: bfloat16 [32, 1024, 512], P('ep')
- w_up: bfloat16 [32, 1024, 512], P('ep')
- w_down: bfloat16 [32, 512, 1024], P('ep')
- d_out: bfloat16 [12288, 1024], P(('dp', 'ep')), parts along dimension 0
- slot_idx: int32 [12288, 8], P(('dp', 'ep')), parts along dimension 0
- expert_id: int32 [12288, 8], P(('dp', 'ep')), parts along dimension 0
- gate_wt: float32 [12288, 8], P(('dp', 'ep')), parts along dimension 0
Outputs:
- output 1: bfloat16 [64, 32, 96, 1024], P('dp', 'ep'), parts along dimension 0
- output 2: bfloat16 [128, 1024, 512], P(('dp', 'ep')), parts along dimension 0
- output 3: bfloat16 [128, 1024, 512], P(('dp', 'ep')), parts along dimension 0
- output 4: bfloat16 [128, 512, 1024], P(('dp', 'ep')), parts along dimension 0
- output 5: float32 [12288, 8], P(('dp', 'ep')), parts along dimension 0
There are 4 independent parts. A program takes and returns all parts, laid end to end along the dimension named above; an argument that names none is the same for every part.
All inputs are finite; a program needn't handle non-finite values.
Results may differ from a plain program's by a relative error of at most 0.00498987.
Values are sent between devices in bfloat16 or wider.
A program may use at most 768 MiB of HBM per device.

v0:
```python
import jax
import jax.numpy as jnp
from jax import lax
from jax.sharding import PartitionSpec as P


def expert_backward(x_rows, out_rows, gate_rows, w_gate, w_up, w_down):
    d_slot = (out_rows.astype(jnp.float32) * gate_rows[..., None]).astype(jnp.bfloat16)
    pre_gate = jnp.einsum('secd,edf->secf', x_rows, w_gate, preferred_element_type=jnp.float32)
    pre_up = jnp.einsum('secd,edf->secf', x_rows, w_up, preferred_element_type=jnp.float32)
    gate_sig = jax.nn.sigmoid(pre_gate)
    silu_gate = pre_gate * gate_sig
    hidden = (silu_gate * pre_up).astype(jnp.bfloat16)
    y_rows = jnp.einsum('secf,efd->secd', hidden, w_down, preferred_element_type=jnp.float32).astype(jnp.bfloat16)
    grad_hidden = jnp.einsum('secd,efd->secf', d_slot, w_down, preferred_element_type=jnp.float32).astype(jnp.bfloat16).astype(jnp.float32)
    grad_pre_gate = (grad_hidden * pre_up * gate_sig * (1.0 + pre_gate * (1.0 - gate_sig))).astype(jnp.bfloat16)
    grad_pre_up = (grad_hidden * silu_gate).astype(jnp.bfloat16)
    grad_x = (jnp.einsum('secf,edf->secd', grad_pre_gate, w_gate, preferred_element_type=jnp.float32) + jnp.einsum('secf,edf->secd', grad_pre_up, w_up, preferred_element_type=jnp.float32)).astype(jnp.bfloat16)
    grad_w_gate = jnp.einsum('secd,secf->edf', x_rows, grad_pre_gate, preferred_element_type=jnp.float32).astype(jnp.bfloat16)
    grad_w_up = jnp.einsum('secd,secf->edf', x_rows, grad_pre_up, preferred_element_type=jnp.float32).astype(jnp.bfloat16)
    grad_w_down = jnp.einsum('secf,secd->efd', hidden, d_slot, preferred_element_type=jnp.float32).astype(jnp.bfloat16)
    gate_grad_rows = jnp.einsum('secd,secd->sec', out_rows, y_rows, preferred_element_type=jnp.float32)
    return grad_x, grad_w_gate, grad_w_up, grad_w_down, gate_grad_rows


def solution(mesh):
    group_size = mesh.shape['ep']

    def local_step(x_disp, w_gate, w_up, w_down, d_out, slot_idx, expert_id, gate_wt):
        e_local, capacity, model_dim = x_disp.shape[1], x_disp.shape[2], x_disp.shape[3]
        tok_dev, top_k = slot_idx.shape
        slot_count = group_size * e_local * capacity
        flat_pos = jnp.where(slot_idx >= 0, expert_id * capacity + slot_idx, slot_count)
        choice_ids = jnp.arange(tok_dev * top_k, dtype=jnp.int32)
        owner_ids = jnp.full((slot_count,), tok_dev * top_k, jnp.int32).at[flat_pos.reshape(-1)].set(choice_ids, mode='drop')
        send_rows = jnp.take(d_out, owner_ids // top_k, axis=0, mode='fill', fill_value=0).reshape(group_size, e_local, capacity, model_dim)
        send_gates = jnp.take(gate_wt.reshape(-1), owner_ids, mode='fill', fill_value=0).reshape(group_size, e_local, capacity)
        out_rows = lax.all_to_all(send_rows, 'ep', 0, 0, tiled=True)
        gate_rows = lax.all_to_all(send_gates, 'ep', 0, 0, tiled=True)
        grad_x, grad_w_gate, grad_w_up, grad_w_down, gate_grad_rows = expert_backward(x_disp, out_rows, gate_rows, w_gate, w_up, w_down)
        back_rows = lax.all_to_all(gate_grad_rows, 'ep', 0, 0, tiled=True)
        grad_gate = jnp.take(back_rows.reshape(-1), flat_pos, mode='fill', fill_value=0)
        return grad_x, grad_w_gate, grad_w_up, grad_w_down, grad_gate

    token_place = P(('dp', 'ep'), None)
    weight_place = P('ep', None, None)
    slot_place = P('dp', 'ep', None, None)
    grad_place = P(('dp', 'ep'), None, None)
    return jax.shard_map(local_step, mesh=mesh,
                         in_specs=(slot_place, weight_place, weight_place, weight_place, token_place, token_place, token_place, token_place),
                         out_specs=(slot_place, grad_place, grad_place, grad_place, token_place),
                         check_vma=False)
```

profile of v0, /device:TPU:21, one launch (start us, length us, event | category | flops | bytes accessed | tf_op | source)
XLA Modules:
  0.0 313.7 jit_solution(13480094049610727896)
XLA Ops:
  0.6 0.0 copy-start
  0.6 0.9 compare_select_fusion.2
  1.5 0.1 copy.54
  1.6 0.1 reshape.75
  1.8 6.2 %scatter_custom_fusion = s32[3072]{0:T(1024)S(1)} fusion(s32[1536]{0:T(1024)S(1)} %fusion.43, s32[1536]{0:T(1024)S(1)} %iota.3, s32[]{:T(128)} %constant.40.clone.1), kind=kCustom, calls=%fused_computation.68 | custom fusion | bytes 12292 | tf_op jit(solution)/shard_map/scatter | solution.py:35
  8.0 0.8 copy.55
  8.8 0.1 reshape.76
  8.9 0.0 copy-start.2
  9.0 17.4 %gather_fusion.1 = f32[3072]{0:T(1024)S(1)} fusion(f32[1536]{0:T(1024)S(1)} %reshape.76, s32[3072]{0:T(1024)S(1)} %get-tuple-element.30), kind=kCustom, calls=%fused_computation.1 | custom fusion | bytes 36864 | tf_op jit(solution)/shard_map/jit(_take)/gather | solution.py:37
  26.4 0.7 select_n.56
  27.1 10.7 %all-to-all-start.1 = ((f32[16,2,96]{2,1,0:T(2,128)}), f32[16,2,96]{2,1,0:T(2,128)S(1)}, u32[]{:S(2)}, u32[]{:S(2)}) async-start(f32[16,2,96]{2,1,0:T(2,128)} %select_n.56), calls=%async_computation.1 | async-start | bytes 32768 | tf_op jit(solution)/shard_map/all_to_all | solution.py:39
  37.8 0.1 broadcast_in_dim.41
  37.9 0.0 copy-done.2
  37.9 13.9 %gather_fusion = bf16[3072,1024]{1,0:T(8,128)(2,1)} fusion(bf16[192,1024]{1,0:T(8,128)(2,1)S(1)} %copy-done.2, s32[3072]{0:T(1024)S(1)} %get-tuple-element.29), kind=kCustom, calls=%fused_computation | custom fusion | bytes 12595200 | tf_op jit(solution)/shard_map/jit(_take)/gather | solution.py:36
  51.8 6.6 %broadcast_select_fusion = bf16[16,2,96,1024]{3,2,1,0:T(8,128)(2,1)} fusion(bf16[16,2,96,1024]{3,2,1,0:T(8,128)(2,1)} %bitcast.92, pred[16,2,96]{2,1,0:T(4,128)(4,1)S(1)} %broadcast_in_dim.41), kind=kLoop, calls=%fused_computation.23 | loop fusion | flops 3145728 | bytes 12585984 | tf_op jit(solution)/shard_map/jit(_take)/select_n | solution.py:36
  58.4 0.0 all-to-all-done.1
  58.4 7.2 %all-to-all-start = ((bf16[16,2,96,1024]{3,2,1,0:T(8,128)(2,1)}), bf16[16,2,96,1024]{3,2,1,0:T(8,128)(2,1)}, u32[]{:S(2)}, u32[]{:S(2)}) async-start(bf16[16,2,96,1024]{3,2,1,0:T(8,128)(2,1)} %broadcast_select_fusion), calls=%async_computation | async-start | bytes 12582912 | tf_op jit(solution)/shard_map/all_to_all | solution.py:38
  65.7 0.1 copy.62
  65.8 0.1 reshape.96
  65.9 9.6 %fusion.18 = f32[2,512,16,96]{1,3,2,0:T(8,128)} fusion(bf16[16,2,96,1024]{3,2,1,0:T(8,128)(2,1)} %param.8, bf16[2,1024,512]{2,1,0:T(8,128)(2,1)} %param.9), kind=kOutput, calls=%fused_computation.35 | convolution fusion | flops 3221225472 | bytes 14680064 | tf_op jit(solution)/shard_map/secd,edf->secf/dot_general | solution.py:9
  75.5 131.4 %all-to-all-done = bf16[16,2,96,1024]{3,2,1,0:T(8,128)(2,1)} async-done(((bf16[16,2,96,1024]{3,2,1,0:T(8,128)(2,1)}), bf16[16,2,96,1024]{3,2,1,0:T(8,128)(2,1)}, u32[]{:S(2)}, u32[]{:S(2)}) %all-to-all-start) | async-done | bytes 6291488 | tf_op jit(solution)/shard_map/all_to_all | solution.py:38
  206.8 0.0 slice-start
  206.8 6.5 %fusion.22 = bf16[2,16,96,512]{3,2,1,0:T(8,128)(2,1)S(1)} fusion(bf16[2,512,1024]{2,1,0:T(8,128)(2,1)} %param.11, f32[16,2,96]{2,1,0:T(2,128)S(1)} %all-to-all-done.1, bf16[16,2,96,1024]{3,2,1,0:T(8,128)(2,1)} %all-to-all-done), kind=kOutput, calls=%fused_computation.39 | convolution fusion | flops 3232235520 | bytes 11546624 | tf_op jit(solution)/shard_map/secd,efd->secf/dot_general | solution.py:15
  213.3 0.0 copy-start.7
  213.3 1.6 copy-done.7
  214.9 0.0 slice-start.1
  214.9 9.6 %fusion.28 = bf16[2,1024,512]{1,2,0:T(8,128)(2,1)} fusion(bf16[16,2,96,1024]{3,2,1,0:T(8,128)(2,1)} %param.8, bf16[2,16,96,512]{3,2,1,0:T(8,128)(2,1)S(1)} %fusion.22, f32[2,512,16,96]{1,3,2,0:T(8,128)} %fusion.18), kind=kOutput, calls=%fused_computation.41 | convolution fusion | flops 3233284096 | bytes 17825792 | tf_op jit(solution)/shard_map/secd,secf->edf/dot_general | solution.py:20
  224.5 0.0 copy-done
  224.5 0.0 slice-done
  224.6 0.0 slice-done.1
  224.6 0.0 copy-start.4
  224.6 9.5 %fusion.8 = (bf16[16,2,96,512]{3,2,0,1:T(8,128)(2,1)S(1)}, bf16[16,2,96,512]{3,2,0,1:T(8,128)(2,1)}) fusion(f32[2,512,16,96]{1,3,2,0:T(8,128)} %fusion.18, bf16[2,16,96,512]{3,2,1,0:T(8,128)(2,1)} %copy-done.7, bf16[16,2,96,1024]{3,2,1,0:T(8,128)(2,1)S(1)} %bitcast.94, bf16[2,1024,512]{2,1,0:T(8,128)(2,1)S(1)} %copy-done), kind=kOutput, calls=%fused_computation.20 | convolution fusion | flops 3243245568 | bytes 24117248 | tf_op jit(solution)/shard_map/secd,edf->secf/dot_general | solution.py:10
  234.1 0.0 copy-start.6
  234.1 0.0 copy-done.4
  234.1 6.9 %multiply_reduce_fusion = f32[16,2,96]{2,0,1:T(8,128)S(1)} fusion(bf16[16,2,96,512]{3,2,0,1:T(8,128)(2,1)S(1)} %get-tuple-element.27, bf16[2,512,1024]{2,1,0:T(8,128)(2,1)S(1)} %copy-done.4, bf16[16,2,96,1024]{3,2,1,0:T(8,128)(2,1)} %all-to-all-done), kind=kOutput, calls=%fused_computation.4 | convolution fusion | flops 3236951040 | bytes 11546624 | tf_op jit(solution)/shard_map/secf,efd->secd/dot_general | solution.py:14
  241.0 0.0 copy-done.6
  241.0 0.6 copy.77
  241.6 8.9 %all-to-all-start.2 = ((f32[16,2,96]{2,1,0:T(2,128)}), f32[16,2,96]{2,1,0:T(2,128)S(1)}, u32[]{:S(2)}, u32[]{:S(2)}) async-start(f32[16,2,96]{2,1,0:T(2,128)} %copy.77), calls=%async_computation.2 | async-start | bytes 32768 | tf_op jit(solution)/shard_map/all_to_all | solution.py:41
  250.6 10.5 %fusion.29 = f32[2,16,96,1024]{3,2,1,0:T(8,128)} fusion(bf16[16,2,96,512]{3,2,0,1:T(8,128)(2,1)} %get-tuple-element.28, bf16[2,1024,512]{2,1,0:T(8,128)(2,1)} %param.9), kind=kOutput, calls=%fused_computation.42 | convolution fusion | flops 3221225472 | bytes 17825792 | tf_op jit(solution)/shard_map/secf,edf->secd/dot_general | solution.py:18
  261.1 13.7 %fusion = bf16[16,2,96,1024]{3,2,0,1:T(8,128)(2,1)} fusion(f32[2,16,96,1024]{3,2,1,0:T(8,128)} %fusion.29, bf16[2,1024,512]{2,1,0:T(8,128)(2,1)S(1)} %copy-done, bf16[2,16,96,512]{3,2,1,0:T(8,128)(2,1)} %copy-done.7, f32[2,512,16,96]{1,3,2,0:T(8,128)} %fusion.18), kind=kOutput, calls=%fused_computation.7 | convolution fusion | flops 3238526976 | bytes 30408704 | tf_op jit(solution)/shard_map/secf,edf->secd/dot_general | solution.py:18
  274.8 0.0 copy-start.5
  274.8 8.8 %bitcast_convert_fusion = bf16[2,512,1024]{2,1,0:T(8,128)(2,1)} fusion(bf16[16,2,96,512]{3,2,0,1:T(8,128)(2,1)} %copy-done.6, f32[16,2,96]{2,1,0:T(2,128)S(1)} %all-to-all-done.1, bf16[16,2,96,1024]{3,2,1,0:T(8,128)(2,1)} %all-to-all-done), kind=kOutput, calls=%fused_computation.28 | convolution fusion | flops 3231711232 | bytes 11546624 | tf_op jit(solution)/shard_map/secf,secd->efd/dot_general | solution.py:21
  283.7 0.0 copy-done.5
  283.7 0.0 copy-start.3
  283.7 7.6 %fusion.27 = bf16[2,1024,512]{1,2,0:T(8,128)(2,1)} fusion(bf16[16,2,96,512]{3,2,0,1:T(8,128)(2,1)S(1)} %copy-done.5, bf16[16,2,96,1024]{3,2,1,0:T(8,128)(2,1)} %param.8), kind=kOutput, calls=%fused_computation.40 | convolution fusion | flops 3222274048 | bytes 11534336 | tf_op jit(solution)/shard_map/secd,secf->edf/dot_general | solution.py:19
  291.3 0.0 copy-done.3
  291.3 2.5 copy.66
  293.8 3.9 %copy.65 = bf16[2,1024,512]{2,1,0:T(8,128)(2,1)} copy(bf16[2,1024,512]{1,2,0:T(8,128)(2,1)} %fusion.27) | data formatting | bytes 4194304
  297.8 6.6 %copy.64 = bf16[16,2,96,1024]{3,2,1,0:T(8,128)(2,1)} copy(bf16[16,2,96,1024]{3,2,0,1:T(8,128)(2,1)} %fusion) | data formatting | bytes 12582912
  304.4 0.0 all-to-all-done.2
  304.4 0.1 reshape.77
  304.5 0.0 copy-start.1
  304.5 8.4 %gather_fusion.2 = f32[1536]{0:T(1024)S(1)} fusion(f32[3072]{0:T(1024)S(1)} %reshape.77, s32[2048]{0:T(1024)S(1)} %pad_clamp_fusion), kind=kCustom, calls=%fused_computation.2 | custom fusion | bytes 18432 | tf_op jit(solution)/shard_map/jit(_take)/gather | solution.py:42
  312.9 0.1 reshape.95
  313.0 0.1 copy.63
  313.0 0.6 and_select_fusion.1
  313.7 0.0 copy-done.1
  (7 shorter events, 0.1 us)
Async XLA Ops:
  0.6 223.9 %copy-start = (bf16[2,1024,512]{2,1,0:T(8,128)(2,1)S(1)}, bf16[2,1024,512]{2,1,0:T(8,128)(2,1)}, u32[]{:S(2)}) copy-start(bf16[2,1024,512]{2,1,0:T(8,128)(2,1)} %param.10) | copy-start | bytes 6291460
  8.9 29.0 %copy-start.2 = (bf16[192,1024]{1,0:T(8,128)(2,1)S(1)}, bf16[192,1024]{1,0:T(8,128)(2,1)}, u32[]{:S(2)}) copy-start(bf16[192,1024]{1,0:T(8,128)(2,1)} %param.12) | copy-start | bytes 1179652
  27.1 31.3 %all-to-all-start.1 = ((f32[16,2,96]{2,1,0:T(2,128)}), f32[16,2,96]{2,1,0:T(2,128)S(1)}, u32[]{:S(2)}, u32[]{:S(2)}) async-start(f32[16,2,96]{2,1,0:T(2,128)} %select_n.56), calls=%async_computation.1 | async-start | bytes 32768 | tf_op jit(solution)/shard_map/all_to_all | solution.py:39
  58.4 148.4 %all-to-all-start = ((bf16[16,2,96,1024]{3,2,1,0:T(8,128)(2,1)}), bf16[16,2,96,1024]{3,2,1,0:T(8,128)(2,1)}, u32[]{:S(2)}, u32[]{:S(2)}) async-start(bf16[16,2,96,1024]{3,2,1,0:T(8,128)(2,1)} %broadcast_select_fusion), calls=%async_computation | async-start | bytes 12582912 | tf_op jit(solution)/shard_map/all_to_all | solution.py:38
  206.8 17.7 %slice-start = ((s8[6291456]{0:T(1024)(128)(4,1)}), s8[4194304]{0:T(1024)(128)(4,1)S(1)}, s32[]{:S(2)}) async-start(s8[6291456]{0:T(1024)(128)(4,1)} %bitcast.93), calls=%async_computation.3 | async-start | bytes 8388608
  213.3 1.6 copy-start.7
  214.9 9.6 %slice-start.1 = ((s8[6291456]{0:T(1024)(128)(4,1)}), s8[2097152]{0:T(1024)(128)(4,1)S(1)}, s32[]{:S(2)}) async-start(s8[6291456]{0:T(1024)(128)(4,1)} %bitcast.93), calls=%async_computation.4 | async-start | bytes 4194304
  224.6 9.6 %copy-start.4 = (bf16[2,512,1024]{2,1,0:T(8,128)(2,1)S(1)}, bf16[2,512,1024]{2,1,0:T(8,128)(2,1)}, u32[]{:S(2)}) copy-start(bf16[2,512,1024]{2,1,0:T(8,128)(2,1)} %param.11) | copy-start | bytes 6291460
  234.1 6.9 %copy-start.6 = (bf16[16,2,96,512]{3,2,0,1:T(8,128)(2,1)}, bf16[16,2,96,512]{3,2,0,1:T(8,128)(2,1)S(1)}, u32[]{:S(2)}) copy-start(bf16[16,2,96,512]{3,2,0,1:T(8,128)(2,1)S(1)} %get-tuple-element.27) | copy-start | bytes 9437188
  241.6 62.7 %all-to-all-start.2 = ((f32[16,2,96]{2,1,0:T(2,128)}), f32[16,2,96]{2,1,0:T(2,128)S(1)}, u32[]{:S(2)}, u32[]{:S(2)}) async-start(f32[16,2,96]{2,1,0:T(2,128)} %copy.77), calls=%async_computation.2 | async-start | bytes 32768 | tf_op jit(solution)/shard_map/all_to_all | solution.py:41
  274.8 8.8 %copy-start.5 = (bf16[16,2,96,512]{3,2,0,1:T(8,128)(2,1)S(1)}, bf16[16,2,96,512]{3,2,0,1:T(8,128)(2,1)}, u32[]{:S(2)}) copy-start(bf16[16,2,96,512]{3,2,0,1:T(8,128)(2,1)} %get-tuple-element.28) | copy-start | bytes 9437188
  283.7 7.6 %copy-start.3 = (bf16[2,1024,512]{1,2,0:T(8,128)(2,1)S(1)}, bf16[2,1024,512]{1,2,0:T(8,128)(2,1)}, u32[]{:S(2)}) copy-start(bf16[2,1024,512]{1,2,0:T(8,128)(2,1)} %fusion.28) | copy-start | bytes 6291460
  304.5 9.2 %copy-start.1 = (bf16[2,1024,512]{2,1,0:T(8,128)(2,1)S(1)}, bf16[2,1024,512]{2,1,0:T(8,128)(2,1)}, u32[]{:S(2)}) copy-start(bf16[2,1024,512]{2,1,0:T(8,128)(2,1)} %param.10) | copy-start | bytes 6291460
where the time goes:
time: 314 us
  waiting for transfers between devices  131 us (42%)
  matrix products  82.8 us (26%)
  local copies, waits for them, and re-layouts  63.6 us (20%)
  starting transfers between devices  26.9 us (9%)
  other arithmetic  8.19 us (3%)
    all_to_all x1, waiting for transfers between devices, local_step(): out_rows = lax.all_to_all(send_rows, 'ep', 0, 0, tiled=True)  131 us
    gather x1, local copies, waits for them, and re-layouts, local_step(): jnp.take(gate_wt.reshape(-1), owner_ids, mode='fill', fill_value=0)  17.4 us
    unnamed x24, local copies, waits for them, and re-layouts  15.6 us
    gather x1, local copies, waits for them, and re-layouts, local_step(): jnp.take(d_out, owner_ids // top_k, axis=0, mode='fill', fill_value=0)  13.9 us
    dot_general x1, matrix products, expert_backward(): jnp.einsum('secf,edf->secd', grad_pre_up, w_up, preferred_element_type=jn...  13.7 us
    all_to_all x1, starting transfers between devices, local_step(): gate_rows = lax.all_to_all(send_gates, 'ep', 0, 0, tiled=True)  10.7 us
    dot_general x1, matrix products, expert_backward(): jnp.einsum('secf,edf->secd', grad_pre_gate, w_gate, preferred_element_typ...  10.5 us
    dot_general x1, matrix products, expert_backward(): jnp.einsum('secd,secf->edf', x_rows, grad_pre_up, preferred_element_type=...  9.61 us
  transfers between devices with their start and end apart: 3, of which 1 were waited for; matrix products, arithmetic and copies ran while one was open for 27% of the time, Pallas kernels for 0%

commit v1 on v0

v1 whole, which is shorter than its diff:
```python
import functools

import jax
import jax.numpy as jnp
from jax import lax
from jax.experimental import pallas as pl
from jax.experimental.pallas import tpu as pltpu
from jax.sharding import PartitionSpec as P

F32 = jnp.float32
BF16 = jnp.bfloat16
MXU = 256


def dot(a, b, ca, cb):
    return lax.dot_general(a, b, (((ca,), (cb,)), ((), ())), preferred_element_type=F32)


def peers(n):
    me = lax.axis_index('ep')
    chips = n // 2
    z, core = me // 2, me % 2
    sgn = 1 - 2 * core
    sib = z * 2 + 1 - core
    nxt = ((z + sgn + chips) % chips) * 2 + core

    def src(k):
        p, side = k // 2, k % 2
        dist, blk = (p + 1) // 2, (p + 1) % 2
        chip = (z + chips - sgn * (1 - 2 * side) * dist) % chips
        other = (side + blk) % 2
        ring_core = jnp.where(p == 0, (core + side) % 2, (core + other) % 2)
        return chip * 2 + ring_core

    return me, sib, nxt, src


def main_kernel(n, x_hbm, wg_hbm, wu_hbm, wd_hbm, do_hbm, slot_ref, eid_ref, gate_ref,
                ybuf, wgu, wd, gg_out,
                gbuf, xbuf, pbuf, qbuf, hbuf, dab, acc_gu, acc_d, rt_src, rt_dst, gg_src, gg_dst,
                x_sem, w_sem, g_sem, ring_s, ring_r, sib_s, sib_r, own_s, own_r,
                rt_s, rt_r, gg_s, gg_r):
    e_loc, cap, dim = x_hbm.shape[1], x_hbm.shape[2], x_hbm.shape[3]
    ffn = wd_hbm.shape[1]
    tok = do_hbm.shape[0]
    half = tok // 2
    rows = n * cap
    pairs = n // 2
    steps = 2 * (pairs - 1)
    me, sib, nxt, src = peers(n)

    def remote(s, d, ss, rs, dev):
        return pltpu.make_async_remote_copy(src_ref=s, dst_ref=d, send_sem=ss, recv_sem=rs,
                                            device_id={'ep': dev}, device_id_type=pl.DeviceIdType.MESH)

    barrier = pltpu.get_barrier_semaphore()

    @pl.loop(1, n)
    def _(i):
        pl.semaphore_signal(barrier, inc=1, device_id={'ep': (me + i) % n}, device_id_type=pl.DeviceIdType.MESH)

    own_load = pltpu.make_async_copy(do_hbm, gbuf.at[0], g_sem)
    own_load.start()

    def x_load(k):
        r = pl.ds(pl.multiple_of(k * cap, 32), cap)
        return pltpu.make_async_copy(x_hbm.at[src(k)], xbuf.at[:, r, :], x_sem.at[k])

    def w_loads(e):
        return (pltpu.make_async_copy(wg_hbm.at[e], wgu.at[e, :, pl.ds(0, ffn)], w_sem.at[e, 0]),
                pltpu.make_async_copy(wu_hbm.at[e], wgu.at[e, :, pl.ds(ffn, ffn)], w_sem.at[e, 1]),
                pltpu.make_async_copy(wd_hbm.at[e], wd.at[e], w_sem.at[e, 2]))

    tile_src = 4
    for k in range(tile_src):
        x_load(k).start()
    for e in range(e_loc):
        for c in w_loads(e):
            c.start()
    for k in range(tile_src, n):
        x_load(k).start()

    slot1 = slot_ref[...].astype(F32) + 1.0
    eid = eid_ref[...]
    gate = gate_ref[...]
    for e in range(n * e_loc):
        hit = eid == e
        rt_src[e // e_loc, pl.ds(e % e_loc, 1), :] = jnp.sum(jnp.where(hit, slot1, 0.0), axis=0, keepdims=True) - 1.0
        rt_src[e // e_loc, pl.ds(e_loc + e % e_loc, 1), :] = jnp.sum(jnp.where(hit, gate, 0.0), axis=0, keepdims=True)

    own_load.wait()
    pl.semaphore_wait(barrier, n - 1)

    def chunk(k, m):
        return gbuf.at[k, pl.ds(pl.multiple_of((m % 2) * half, 32), half), :]

    def ring_copy(m, k_from):
        return remote(chunk(k_from, m), chunk(2 + 2 * (m // 2), m), ring_s.at[m], ring_r.at[m], nxt)

    def sib_copy(m):
        k = 2 + 2 * (m // 2)
        return remote(chunk(k, m), chunk(k + 1, m), sib_s.at[m], sib_r.at[m], sib)

    own_copy = remote(gbuf.at[0], gbuf.at[1], own_s, own_r, sib)
    for m in range(2):
        ring_copy(m, 0).start()
    own_copy.start()

    def comm(m):
        k = 2 + 2 * (m // 2)
        ring_copy(m, k).wait_recv()
        if isinstance(m, int):
            if m + 4 < steps:
                ring_copy(m + 4, k).start()
        else:
            @pl.when(m + 4 < steps)
            def _():
                ring_copy(m + 4, k).start()
        sib_copy(m).start()

    def route_copy(i):
        return remote(rt_src.at[(me + i) % n], rt_dst.at[me], rt_s.at[i], rt_r.at[i], (me + i) % n)

    tile = tile_src * cap
    n_tiles = rows // tile

    def phase_a(e, t):
        r = pl.ds(pl.multiple_of(t * tile, 128), tile)
        xt = xbuf[e, r, :]
        for c in range(ffn // MXU):
            cols = pl.ds(c * MXU, MXU)
            a = dot(xt, wgu[e, :, cols], 1, 0)
            b = dot(xt, wgu[e, :, pl.ds(ffn + c * MXU, MXU)], 1, 0)
            sg = jax.nn.sigmoid(a)
            silu = a * sg
            hbuf[e, r, cols] = (silu * b).astype(BF16)
            qbuf[e, r, cols] = silu
            pbuf[e, r, cols] = b * sg * (1.0 + a * (1.0 - sg))
        ht = hbuf[e, r, :]
        for c in range(dim // MXU):
            cols = pl.ds(c * MXU, MXU)
            ybuf[e, r, cols] = dot(ht, wd[e, :, cols], 1, 0).astype(BF16)

    def a_step(i):
        e, t = i % e_loc, i // e_loc

        @pl.when(e == 0)
        def _():
            for j in range(tile_src):
                x_load(t * tile_src + j).wait()

        @pl.when(t == 0)
        def _():
            for c in w_loads(e):
                c.wait()

        phase_a(e, t)

    a_step(0)
    own_copy.wait_recv()
    for m in range(2, 4):
        ring_copy(m, 1).start()

    @pl.loop(1, n)
    def _(i):
        route_copy(i).start()
    rt_dst[me] = rt_src[me]

    @pl.loop(1, n_tiles * e_loc)
    def _(i):
        a_step(i)

        @pl.when(i % 3 != 0)
        def _():
            comm((2 * i - 1) // 3)
    done_m = (2 * (n_tiles * e_loc - 1) - 1) // 3 + 1

    @pl.loop(1, n)
    def _(i):
        route_copy(i).wait_recv()

    slot_no = lax.broadcasted_iota(jnp.int32, (cap, tok), 0).astype(F32)

    def select_rows(k):
        s = src(k)
        r = pl.ds(pl.multiple_of(k * cap, 32), cap)
        rt = rt_dst[s]
        hits = [slot_no == rt[e:e + 1, :] for e in range(e_loc)]
        gcols = [jnp.sum(jnp.where(hits[e], rt[e_loc + e:e_loc + e + 1, :], 0.0), axis=1, keepdims=True)
                 for e in range(e_loc)]
        onehot = jnp.concatenate([jnp.where(h, 1.0, 0.0).astype(BF16) for h in hits], axis=0)
        dots = [jnp.zeros((cap, 1), F32) for _ in range(e_loc)]
        for c in range(dim // MXU):
            cols = pl.ds(c * MXU, MXU)
            o = dot(onehot, gbuf[k, :, cols], 1, 0)
            for e in range(e_loc):
                oe = o[e * cap:(e + 1) * cap, :]
                dots[e] = dots[e] + jnp.sum(oe * ybuf[e, r, cols].astype(F32), axis=1, keepdims=True)
                ybuf[e, r, cols] = (oe * gcols[e]).astype(BF16)
        for e in range(e_loc):
            gg_src[k, pl.ds(e, 1), :] = jnp.sum(jnp.where(hits[e], dots[e], 0.0), axis=0, keepdims=True)

    def gg_copy(k):
        s = src(k)
        off = (s - me + n) % n
        return remote(gg_src.at[k], gg_dst.at[me], gg_s.at[off], gg_r.at[off], s)

    def gg_send(k0, k1):
        for k in range(k0, k1):
            if k == 0:
                gg_dst[me] = gg_src[0]
            else:
                gg_copy(k).start()

    def hidden_grads(e, r0, r1):
        r = pl.ds(r0, r1 - r0)
        dy = ybuf[e, r, :]
        for c in range(ffn // MXU):
            cols = pl.ds(c * MXU, MXU)
            dh = dot(dy, wd[e, cols, :], 1, 1).astype(BF16).astype(F32)
            dab[e, r, cols] = (dh * pbuf[e, r, cols]).astype(BF16)
            dab[e, r, pl.ds(ffn + c * MXU, MXU)] = (dh * qbuf[e, r, cols]).astype(BF16)

    def weight_grad(lhs, rhs, acc, out, w0, w1, e, t):
        cols = pl.ds(pl.multiple_of(t * MXU, MXU), MXU)
        r = pl.ds(w0, w1 - w0)
        for c in range(dim // (2 * MXU)):
            oc = pl.ds(c * 2 * MXU, 2 * MXU)
            g = dot(lhs[e, r, cols], rhs[e, r, oc], 0, 0)
            if w0 > 0:
                g = g + acc[e, cols, oc]
            if w1 == rows:
                out[e, cols, oc] = g.astype(BF16)
            else:
                acc[e, cols, oc] = g

    def x_grad(e, r0, r1):
        r = pl.ds(r0, r1 - r0)
        da = dab[e, r, :]
        for c in range(dim // MXU):
            ybuf[e, r, pl.ds(c * MXU, MXU)] = dot(da, wgu[e, pl.ds(c * MXU, MXU), :], 1, 1).astype(BF16)

    next_m = [done_m]

    def comm_next(count=1):
        for _ in range(count):
            if next_m[0] < steps:
                comm(next_m[0])
                next_m[0] += 1

    stages = [(0, 3, 0, 512), (3, 5, 512, 768), (5, 7, 768, 1280), (7, 8, 1280, 1536)]
    for p0, p1, w0, w1 in stages:
        need = 2 * (p1 - 1)
        if next_m[0] < need:
            comm_next(need - next_m[0])
        for p in range(max(p0, 1), p1):
            for m in (2 * p - 2, 2 * p - 1):
                sib_copy(m).wait_recv()

        @pl.loop(2 * p0, 2 * p1)
        def _(k):
            select_rows(k)
        comm_next()

        @pl.loop(0, e_loc)
        def _(e):
            hidden_grads(e, 2 * p0 * cap, 2 * p1 * cap)
        gg_send(2 * p0, 2 * p1)
        comm_next()

        @pl.loop(0, e_loc * (ffn // MXU))
        def _(i):
            weight_grad(hbuf, ybuf, acc_d, wd, w0, w1, i % e_loc, i // e_loc)
        comm_next()

        @pl.loop(0, e_loc)
        def _(e):
            x_grad(e, w0, w1)
        comm_next()

        @pl.loop(0, e_loc * (dim // MXU))
        def _(i):
            weight_grad(xbuf, dab, acc_gu, wgu, w0, w1, i % e_loc, i // e_loc)
        comm_next()

    @pl.loop(1, n)
    def _(k):
        gg_copy(k).wait_recv()
        gg_copy(k).wait_send()
        route_copy(k).wait_send()
    for m in range(steps):
        ring_copy(m, 0).wait_send()
        sib_copy(m).wait_send()
    own_copy.wait_send()
    gg_out[...] = gg_dst[...]


def write_kernel(n, ybuf, wgu, wd, gg, eid_ref, gx_hbm, gwg_hbm, gwu_hbm, gwd_hbm, gate_out, y_sem, w_sem):
    cap = gx_hbm.shape[2]
    e_loc, ffn = wd.shape[0], wd.shape[1]
    _, _, _, src = peers(n)
    copies = [pltpu.make_async_copy(wgu.at[:, :, pl.ds(0, ffn)], gwg_hbm, w_sem.at[0]),
              pltpu.make_async_copy(wgu.at[:, :, pl.ds(ffn, ffn)], gwu_hbm, w_sem.at[1]),
              pltpu.make_async_copy(wd, gwd_hbm, w_sem.at[2])]
    for k in range(n):
        copies.append(pltpu.make_async_copy(ybuf.at[:, pl.ds(k * cap, cap), :], gx_hbm.at[src(k)], y_sem.at[k]))
    for c in copies:
        c.start()
    eid = eid_ref[...]
    out = jnp.zeros(eid.shape, F32)
    for e in range(n * e_loc):
        out = out + jnp.where(eid == e, gg[e // e_loc, pl.ds(e % e_loc, 1), :], 0.0)
    gate_out[...] = out
    for c in copies:
        c.wait()


def solution(mesh):
    n = mesh.shape['ep']

    def local_step(x_disp, w_gate, w_up, w_down, d_out, slot_idx, expert_id, gate_wt):
        _, e_loc, cap, dim = x_disp.shape
        ffn = w_down.shape[1]
        tok, top_k = slot_idx.shape
        rows = n * cap
        steps = 2 * (n // 2 - 1)
        slot_t, eid_t, gate_t = slot_idx.T, expert_id.T, gate_wt.T
        vmem = pl.BlockSpec(memory_space=pltpu.VMEM)
        hbm = pl.BlockSpec(memory_space=pl.ANY)
        dma = pltpu.SemaphoreType.DMA
        ybuf, wgu, wd, gg = pl.pallas_call(
            functools.partial(main_kernel, n),
            out_shape=(pltpu.VMEM((e_loc, rows, dim), BF16),
                       pltpu.VMEM((e_loc, dim, 2 * ffn), BF16),
                       pltpu.VMEM((e_loc, ffn, dim), BF16),
                       pltpu.VMEM((n, e_loc, tok), F32)),
            in_specs=[hbm] * 5 + [vmem] * 3,
            out_specs=[vmem] * 4,
            scratch_shapes=[
                pltpu.VMEM((n, tok, dim), BF16),
                pltpu.VMEM((e_loc, rows, dim), BF16),
                pltpu.VMEM((e_loc, rows, ffn), F32),
                pltpu.VMEM((e_loc, rows, ffn), F32),
                pltpu.VMEM((e_loc, rows, ffn), BF16),
                pltpu.VMEM((e_loc, rows, 2 * ffn), BF16),
                pltpu.VMEM((e_loc, dim, 2 * ffn), F32),
                pltpu.VMEM((e_loc, ffn, dim), F32),
                pltpu.VMEM((n, 2 * e_loc, tok), F32),
                pltpu.VMEM((n, 2 * e_loc, tok), F32),
                pltpu.VMEM((n, e_loc, tok), F32),
                pltpu.VMEM((n, e_loc, tok), F32),
                dma((n,)), dma((e_loc, 3)), dma,
                dma((steps,)), dma((steps,)), dma((steps,)), dma((steps,)), dma, dma,
                dma((n,)), dma((n,)), dma((n,)), dma((n,)),
            ],
            compiler_params=pltpu.CompilerParams(collective_id=0, has_side_effects=True,
                                                 vmem_limit_bytes=49 * 1024 * 1024),
            name='experts',
        )(x_disp, w_gate, w_up, w_down, d_out, slot_t, eid_t, gate_t)
        grad_x, grad_wg, grad_wu, grad_wd, gate_out = pl.pallas_call(
            functools.partial(write_kernel, n),
            out_shape=(jax.ShapeDtypeStruct(x_disp.shape, BF16),
                       jax.ShapeDtypeStruct(w_gate.shape, BF16),
                       jax.ShapeDtypeStruct(w_up.shape, BF16),
                       jax.ShapeDtypeStruct(w_down.shape, BF16),
                       jax.ShapeDtypeStruct((top_k, tok), F32)),
            in_specs=[vmem] * 5,
            out_specs=[hbm] * 4 + [vmem],
            scratch_shapes=[dma((n,)), dma((3,))],
            compiler_params=pltpu.CompilerParams(vmem_limit_bytes=4 * 1024 * 1024),
            name='write_out',
        )(ybuf, wgu, wd, gg, eid_t)
        return grad_x, grad_wg, grad_wu, grad_wd, gate_out.T

    token_place = P(('dp', 'ep'), None)
    weight_place = P('ep', None, None)
    slot_place = P('dp', 'ep', None, None)
    grad_place = P(('dp', 'ep'), None, None)
    return jax.shard_map(local_step, mesh=mesh,
                         in_specs=(slot_place, weight_place, weight_place, weight_place,
                                   token_place, token_place, token_place, token_place),
                         out_specs=(slot_place, grad_place, grad_place, grad_place, token_place),
                         check_vma=False)
```

time: 314 us -> 74.1 us (0.24)
  waiting for transfers between devices: 131 us -> 0 us
  matrix products: 82.8 us -> 0 us
  Pallas kernels: 0 us -> 72.2 us
  local copies, waits for them, and re-layouts: 63.6 us -> 0.01 us
  starting transfers between devices: 26.9 us -> 0 us
  other arithmetic: 8.19 us -> 0 us
    all_to_all x3 -> x0, waiting for transfers between devices: 131 us -> none  [the longest x1 131 us: local_step(): out_rows = lax.all_to_all(send_rows, 'ep', 0, 0, tiled=True)]
    dot_general x9 -> x0, matrix products: 82.8 us -> none  [the longest x1 13.7 us: expert_backward(): jnp.einsum('secf,edf->secd', grad_pre_up, w_up, preferred_element_type=jn...]
    pallas_call x0 -> x2, Pallas kernels: none -> 72.2 us  [the longest x1 66.9 us: local_step(): pl.pallas_call(functools.partial(main_kernel, n), out_shape=(pltpu.VMEM((...]
    gather x5 -> x0, local copies, waits for them, and re-layouts: 39.8 us -> none  [the longest x1 17.4 us: local_step(): jnp.take(gate_wt.reshape(-1), owner_ids, mode='fill', fill_value=0)]
    all_to_all x3 -> x0, starting transfers between devices: 26.9 us -> none  [the longest x1 10.7 us: local_step(): gate_rows = lax.all_to_all(send_gates, 'ep', 0, 0, tiled=True)]
    unnamed x24 -> x2, local copies, waits for them, and re-layouts: 15.6 us -> 0.01 us
    select_n x5 -> x0, other arithmetic: 8.14 us -> none  [the longest x1 6.62 us: local_step(): jnp.take(d_out, owner_ids // top_k, axis=0, mode='fill', fill_value=0)]
    scatter x1 -> x0, local copies, waits for them, and re-layouts: 6.19 us -> none  [local_step(): jnp.full((slot_count,), tok_dev * top_k, jnp.int32).at[flat_pos.reshape(-1)]]
  transfers between devices with their start and end apart: 3 -> 0, of which waited for: 1 -> 0; matrix products, arithmetic and copies ran while one was open for 27% -> 0% of each run, Pallas kernels for 0% -> 0%
where the time goes in v1:
time: 74.1 us; the launch traced here: 72.9 us
  Pallas kernels  72.2 us (97%)
    pallas_call x1, Pallas kernels, local_step(): pl.pallas_call(functools.partial(main_kernel, n), out_shape=(pltpu.VMEM((...  66.9 us
    pallas_call x1, Pallas kernels, local_step(): pl.pallas_call(functools.partial(write_kernel, n), out_shape=(jax.ShapeDt...  5.32 us

profile of v1, /device:TPU:21, one launch (start us, length us, event | category | flops | bytes accessed | tf_op | source)
XLA Modules:
  0.0 72.9 jit_solution(16743061150517403214)
XLA Ops:
  0.6 0.0 copy-start
  0.6 66.9 %experts.1 = (bf16[2,1536,1024]{2,1,0:T(8,128)(2,1)S(1)}, bf16[2,1024,1024]{2,1,0:T(8,128)(2,1)S(1)}, bf16[2,512,1024]{2,1,0:T(8,128)(2,1)S(1)}, f32[16,2,192]{2,1,0:T(2,128)S(1)}) custom-call(bf16[16,2,96,1024]{3,2,1,0:T(8,128)(2,1)} %x_hbm.1, bf16[2,1024,512]{2,1,0:T(8,128)(2,1)} %wg_hbm.1, bf16[2,1024,512]{2,1,0:T(8,128)(2,1)} %wu_hbm.1, ...), custom_call_target="tpu_custom_call" | custom-call | tf_op jit(solution)/shard_map/experts/pallas_call | solution.py:331
  67.6 0.0 copy-done
  67.6 5.3 %write_out.1 = (bf16[16,2,96,1024]{3,2,1,0:T(8,128)(2,1)}, bf16[2,1024,512]{2,1,0:T(8,128)(2,1)}, bf16[2,1024,512]{2,1,0:T(8,128)(2,1)}, bf16[2,512,1024]{2,1,0:T(8,128)(2,1)}, f32[8,192]{1,0:T(8,128)}) custom-call(bf16[2,1536,1024]{2,1,0:T(8,128)(2,1)S(1)} %get-tuple-element.14.ybuf, bf16[2,1024,1024]{2,1,0:T(8,128)(2,1)S(1)} %get-tuple-element.15.wgu, ...), custom_call_target="tpu_custom_call" | custom-call | tf_op jit(solution)/shard_map/write_out/pallas_call | solution.py:360
Async XLA Ops:
  0.6 66.9 %copy-start = (s32[192,8]{0,1:T(8,128)S(1)}, s32[192,8]{0,1:T(8,128)}, u32[]{:S(2)}) copy-start(s32[192,8]{0,1:T(8,128)} %param.14) | copy-start | bytes 18436

commit v2 on v1

--- a/solution.py
+++ b/solution.py
@@ -10,6 +10,7 @@
 F32 = jnp.float32
 BF16 = jnp.bfloat16
 MXU = 256
+LANES = 128
 
 
 def dot(a, b, ca, cb):
@@ -36,8 +37,8 @@
 
 
 def main_kernel(n, x_hbm, wg_hbm, wu_hbm, wd_hbm, do_hbm, slot_ref, eid_ref, gate_ref,
-                ybuf, wgu, wd, gg_out,
-                gbuf, xbuf, pbuf, qbuf, hbuf, dab, acc_gu, acc_d, rt_src, rt_dst, gg_src, gg_dst,
+                ybuf, xbuf, wgu, wd, dab, gg_out,
+                gbuf, pbuf, qbuf, hbuf, acc_gu, acc_d, rt_src, rt_dst, gg_src, gg_dst,
                 x_sem, w_sem, g_sem, ring_s, ring_r, sib_s, sib_r, own_s, own_r,
                 rt_s, rt_r, gg_s, gg_r):
     e_loc, cap, dim = x_hbm.shape[1], x_hbm.shape[2], x_hbm.shape[3]
@@ -74,15 +75,13 @@
     tile_src = 4
     for k in range(tile_src):
         x_load(k).start()
-    for e in range(e_loc):
-        for c in w_loads(e):
-            c.start()
-    for k in range(tile_src, n):
-        x_load(k).start()
-
-    slot1 = slot_ref[...].astype(F32) + 1.0
-    eid = eid_ref[...]
-    gate = gate_ref[...]
+    for c in w_loads(0):
+        c.start()
+
+    pad = ((0, 0), (0, rt_src.shape[2] - tok))
+    slot1 = jnp.pad(slot_ref[...].astype(F32) + 1.0, pad)
+    eid = jnp.pad(eid_ref[...], pad)
+    gate = jnp.pad(gate_ref[...], pad)
     for e in range(n * e_loc):
         hit = eid == e
         rt_src[e // e_loc, pl.ds(e % e_loc, 1), :] = jnp.sum(jnp.where(hit, slot1, 0.0), axis=0, keepdims=True) - 1.0
@@ -141,7 +140,7 @@
             cols = pl.ds(c * MXU, MXU)
             ybuf[e, r, cols] = dot(ht, wd[e, :, cols], 1, 0).astype(BF16)
 
-    def a_step(i):
+    def a_wait(i):
         e, t = i % e_loc, i // e_loc
 
         @pl.when(e == 0)
@@ -154,9 +153,13 @@
             for c in w_loads(e):
                 c.wait()
 
-        phase_a(e, t)
-
-    a_step(0)
+    a_wait(0)
+    for e in range(1, e_loc):
+        for c in w_loads(e):
+            c.start()
+    for k in range(tile_src, n):
+        x_load(k).start()
+    phase_a(0, 0)
     own_copy.wait_recv()
     for m in range(2, 4):
         ring_copy(m, 1).start()
@@ -168,7 +171,8 @@
 
     @pl.loop(1, n_tiles * e_loc)
     def _(i):
-        a_step(i)
+        a_wait(i)
+        phase_a(i % e_loc, i // e_loc)
 
         @pl.when(i % 3 != 0)
         def _():
@@ -179,26 +183,32 @@
     def _(i):
         route_copy(i).wait_recv()
 
-    slot_no = lax.broadcasted_iota(jnp.int32, (cap, tok), 0).astype(F32)
+    wide = rt_dst.shape[2]
+    slot_no = lax.broadcasted_iota(jnp.int32, (cap, wide), 0).astype(F32)
+
+    def lanes_sum(v):
+        parts = [v[:, i:i + LANES] for i in range(0, v.shape[1], LANES)]
+        return functools.reduce(jnp.add, parts)
 
     def select_rows(k):
         s = src(k)
         r = pl.ds(pl.multiple_of(k * cap, 32), cap)
         rt = rt_dst[s]
         hits = [slot_no == rt[e:e + 1, :] for e in range(e_loc)]
-        gcols = [jnp.sum(jnp.where(hits[e], rt[e_loc + e:e_loc + e + 1, :], 0.0), axis=1, keepdims=True)
+        gcols = [jnp.sum(lanes_sum(jnp.where(hits[e], rt[e_loc + e:e_loc + e + 1, :], 0.0)), axis=1, keepdims=True)
                  for e in range(e_loc)]
-        onehot = jnp.concatenate([jnp.where(h, 1.0, 0.0).astype(BF16) for h in hits], axis=0)
-        dots = [jnp.zeros((cap, 1), F32) for _ in range(e_loc)]
+        onehot = jnp.concatenate([jnp.where(h, 1.0, 0.0).astype(BF16)[:, :tok] for h in hits], axis=0)
+        dots = [jnp.zeros((cap, LANES), F32) for _ in range(e_loc)]
         for c in range(dim // MXU):
             cols = pl.ds(c * MXU, MXU)
             o = dot(onehot, gbuf[k, :, cols], 1, 0)
             for e in range(e_loc):
                 oe = o[e * cap:(e + 1) * cap, :]
-                dots[e] = dots[e] + jnp.sum(oe * ybuf[e, r, cols].astype(F32), axis=1, keepdims=True)
+                dots[e] = dots[e] + lanes_sum(oe * ybuf[e, r, cols].astype(F32))
                 ybuf[e, r, cols] = (oe * gcols[e]).astype(BF16)
         for e in range(e_loc):
-            gg_src[k, pl.ds(e, 1), :] = jnp.sum(jnp.where(hits[e], dots[e], 0.0), axis=0, keepdims=True)
+            dot_col = jnp.sum(dots[e], axis=1, keepdims=True)
+            gg_src[k, pl.ds(e, 1), :] = jnp.sum(jnp.where(hits[e], dot_col, 0.0), axis=0, keepdims=True)
 
     def gg_copy(k):
         s = src(k)
@@ -221,18 +231,15 @@
             dab[e, r, cols] = (dh * pbuf[e, r, cols]).astype(BF16)
             dab[e, r, pl.ds(ffn + c * MXU, MXU)] = (dh * qbuf[e, r, cols]).astype(BF16)
 
-    def weight_grad(lhs, rhs, acc, out, w0, w1, e, t):
-        cols = pl.ds(pl.multiple_of(t * MXU, MXU), MXU)
+    def weight_grad(lhs, rhs, acc, out, w0, w1, e):
         r = pl.ds(w0, w1 - w0)
-        for c in range(dim // (2 * MXU)):
-            oc = pl.ds(c * 2 * MXU, 2 * MXU)
-            g = dot(lhs[e, r, cols], rhs[e, r, oc], 0, 0)
-            if w0 > 0:
-                g = g + acc[e, cols, oc]
-            if w1 == rows:
-                out[e, cols, oc] = g.astype(BF16)
-            else:
-                acc[e, cols, oc] = g
+        g = dot(lhs[e, r, :], rhs[e, r, :], 0, 0)
+        if w0 > 0:
+            g = g + acc[e]
+        if w1 == rows:
+            out[e, pl.ds(0, g.shape[0]), :] = g.astype(BF16)
+        else:
+            acc[e] = g
 
     def x_grad(e, r0, r1):
         r = pl.ds(r0, r1 - r0)
@@ -248,6 +255,7 @@
                 comm(next_m[0])
                 next_m[0] += 1
 
+    kept = x_grad_rows(rows)
     stages = [(0, 3, 0, 512), (3, 5, 512, 768), (5, 7, 768, 1280), (7, 8, 1280, 1536)]
     for p0, p1, w0, w1 in stages:
         need = 2 * (p1 - 1)
@@ -257,30 +265,28 @@
             for m in (2 * p - 2, 2 * p - 1):
                 sib_copy(m).wait_recv()
 
-        @pl.loop(2 * p0, 2 * p1)
-        def _(k):
+        for k in range(2 * p0, 2 * p1):
             select_rows(k)
         comm_next()
 
-        @pl.loop(0, e_loc)
-        def _(e):
+        for e in range(e_loc):
             hidden_grads(e, 2 * p0 * cap, 2 * p1 * cap)
         gg_send(2 * p0, 2 * p1)
         comm_next()
 
-        @pl.loop(0, e_loc * (ffn // MXU))
-        def _(i):
-            weight_grad(hbuf, ybuf, acc_d, wd, w0, w1, i % e_loc, i // e_loc)
-        comm_next()
-
         @pl.loop(0, e_loc)
         def _(e):
-            x_grad(e, w0, w1)
+            weight_grad(hbuf, ybuf, acc_d, wd, w0, w1, e)
         comm_next()
 
-        @pl.loop(0, e_loc * (dim // MXU))
-        def _(i):
-            weight_grad(xbuf, dab, acc_gu, wgu, w0, w1, i % e_loc, i // e_loc)
+        if w1 <= kept:
+            for e in range(e_loc):
+                x_grad(e, w0, w1)
+        comm_next()
+
+        @pl.loop(0, e_loc)
+        def _(e):
+            weight_grad(xbuf, dab, acc_gu, xbuf, w0, w1, e)
         comm_next()
 
     @pl.loop(1, n)
@@ -295,21 +301,41 @@
     gg_out[...] = gg_dst[...]
 
 
-def write_kernel(n, ybuf, wgu, wd, gg, eid_ref, gx_hbm, gwg_hbm, gwu_hbm, gwd_hbm, gate_out, y_sem, w_sem):
-    cap = gx_hbm.shape[2]
+def x_grad_rows(rows):
+    return rows // 2
+
+
+def write_kernel(n, ybuf, xbuf, wgu, wd, dab, gg, eid_ref, gx_hbm, gwg_hbm, gwu_hbm, gwd_hbm, gate_out,
+                 obuf, y_sem, w_sem):
+    cap, dim = gx_hbm.shape[2], gx_hbm.shape[3]
     e_loc, ffn = wd.shape[0], wd.shape[1]
+    kept = x_grad_rows(n * cap)
     _, _, _, src = peers(n)
-    copies = [pltpu.make_async_copy(wgu.at[:, :, pl.ds(0, ffn)], gwg_hbm, w_sem.at[0]),
-              pltpu.make_async_copy(wgu.at[:, :, pl.ds(ffn, ffn)], gwu_hbm, w_sem.at[1]),
-              pltpu.make_async_copy(wd, gwd_hbm, w_sem.at[2])]
-    for k in range(n):
-        copies.append(pltpu.make_async_copy(ybuf.at[:, pl.ds(k * cap, cap), :], gx_hbm.at[src(k)], y_sem.at[k]))
+
+    def put(buf, row, k):
+        return pltpu.make_async_copy(buf.at[:, pl.ds(row, cap), :], gx_hbm.at[src(k)], y_sem.at[k])
+
+    copies = [put(ybuf, k * cap, k) for k in range(kept // cap)]
+    copies += [pltpu.make_async_copy(xbuf.at[:, pl.ds(0, dim), pl.ds(0, ffn)], gwg_hbm, w_sem.at[0]),
+               pltpu.make_async_copy(xbuf.at[:, pl.ds(0, dim), pl.ds(ffn, ffn)], gwu_hbm, w_sem.at[1]),
+               pltpu.make_async_copy(wd, gwd_hbm, w_sem.at[2])]
     for c in copies:
         c.start()
+    tile = (n * cap - kept) // 2
+    for t in range(2):
+        for e in range(e_loc):
+            da = dab[e, pl.ds(kept + t * tile, tile), :]
+            for c in range(dim // MXU):
+                obuf[e, pl.ds(t * tile, tile), pl.ds(c * MXU, MXU)] = dot(
+                    da, wgu[e, pl.ds(c * MXU, MXU), :], 1, 1).astype(BF16)
+        for k in range((kept + t * tile) // cap, (kept + (t + 1) * tile) // cap):
+            c = put(obuf, k * cap - kept, k)
+            c.start()
+            copies.append(c)
     eid = eid_ref[...]
     out = jnp.zeros(eid.shape, F32)
     for e in range(n * e_loc):
-        out = out + jnp.where(eid == e, gg[e // e_loc, pl.ds(e % e_loc, 1), :], 0.0)
+        out = out + jnp.where(eid == e, gg[e // e_loc, pl.ds(e % e_loc, 1), pl.ds(0, eid.shape[1])], 0.0)
     gate_out[...] = out
     for c in copies:
         c.wait()
@@ -323,38 +349,39 @@
         ffn = w_down.shape[1]
         tok, top_k = slot_idx.shape
         rows = n * cap
+        wide = pl.cdiv(tok, LANES) * LANES
         steps = 2 * (n // 2 - 1)
         slot_t, eid_t, gate_t = slot_idx.T, expert_id.T, gate_wt.T
         vmem = pl.BlockSpec(memory_space=pltpu.VMEM)
         hbm = pl.BlockSpec(memory_space=pl.ANY)
         dma = pltpu.SemaphoreType.DMA
-        ybuf, wgu, wd, gg = pl.pallas_call(
+        ybuf, xbuf, wgu, wd, dab, gg = pl.pallas_call(
             functools.partial(main_kernel, n),
             out_shape=(pltpu.VMEM((e_loc, rows, dim), BF16),
+                       pltpu.VMEM((e_loc, rows, dim), BF16),
                        pltpu.VMEM((e_loc, dim, 2 * ffn), BF16),
                        pltpu.VMEM((e_loc, ffn, dim), BF16),
-                       pltpu.VMEM((n, e_loc, tok), F32)),
+                       pltpu.VMEM((e_loc, rows, 2 * ffn), BF16),
+                       pltpu.VMEM((n, e_loc, wide), F32)),
             in_specs=[hbm] * 5 + [vmem] * 3,
-            out_specs=[vmem] * 4,
+            out_specs=[vmem] * 6,
             scratch_shapes=[
                 pltpu.VMEM((n, tok, dim), BF16),
-                pltpu.VMEM((e_loc, rows, dim), BF16),
                 pltpu.VMEM((e_loc, rows, ffn), F32),
                 pltpu.VMEM((e_loc, rows, ffn), F32),
                 pltpu.VMEM((e_loc, rows, ffn), BF16),
-                pltpu.VMEM((e_loc, rows, 2 * ffn), BF16),
                 pltpu.VMEM((e_loc, dim, 2 * ffn), F32),
                 pltpu.VMEM((e_loc, ffn, dim), F32),
-                pltpu.VMEM((n, 2 * e_loc, tok), F32),
-                pltpu.VMEM((n, 2 * e_loc, tok), F32),
-                pltpu.VMEM((n, e_loc, tok), F32),
-                pltpu.VMEM((n, e_loc, tok), F32),
+                pltpu.VMEM((n, 2 * e_loc, wide), F32),
+                pltpu.VMEM((n, 2 * e_loc, wide), F32),
+                pltpu.VMEM((n, e_loc, wide), F32),
+                pltpu.VMEM((n, e_loc, wide), F32),
                 dma((n,)), dma((e_loc, 3)), dma,
                 dma((steps,)), dma((steps,)), dma((steps,)), dma((steps,)), dma, dma,
                 dma((n,)), dma((n,)), dma((n,)), dma((n,)),
             ],
             compiler_params=pltpu.CompilerParams(collective_id=0, has_side_effects=True,
-                                                 vmem_limit_bytes=49 * 1024 * 1024),
+                                                 vmem_limit_bytes=39 * 1024 * 1024),
             name='experts',
         )(x_disp, w_gate, w_up, w_down, d_out, slot_t, eid_t, gate_t)
         grad_x, grad_wg, grad_wu, grad_wd, gate_out = pl.pallas_call(
@@ -364,12 +391,12 @@
                        jax.ShapeDtypeStruct(w_up.shape, BF16),
                        jax.ShapeDtypeStruct(w_down.shape, BF16),
                        jax.ShapeDtypeStruct((top_k, tok), F32)),
-            in_specs=[vmem] * 5,
+            in_specs=[vmem] * 7,
             out_specs=[hbm] * 4 + [vmem],
-            scratch_shapes=[dma((n,)), dma((3,))],
-            compiler_params=pltpu.CompilerParams(vmem_limit_bytes=4 * 1024 * 1024),
+            scratch_shapes=[pltpu.VMEM((e_loc, rows - x_grad_rows(rows), dim), BF16), dma((n,)), dma((3,))],
+            compiler_params=pltpu.CompilerParams(vmem_limit_bytes=8 * 1024 * 1024),
             name='write_out',
-        )(ybuf, wgu, wd, gg, eid_t)
+        )(ybuf, xbuf, wgu, wd, dab, gg, eid_t)
         return grad_x, grad_wg, grad_wu, grad_wd, gate_out.T
 
     token_place = P(('dp', 'ep'), None)

time: 74.1 us -> 65.5 us (0.88); the launches traced: 72.9 us -> 65.4 us
  Pallas kernels: 72.2 us -> 64.6 us
    pallas_call x1, Pallas kernels: 66.9 us -> 59.1 us  [local_step(): pl.pallas_call(functools.partial(main_kernel, n), out_shape=(pltpu.VMEM((...]
where the time goes in v2:
time: 65.5 us; the launch traced here: 65.4 us
  Pallas kernels  64.6 us (99%)
  between operations  0.82 us (1%)
    pallas_call x1, Pallas kernels, local_step(): pl.pallas_call(functools.partial(main_kernel, n), out_shape=(pltpu.VMEM((...  59.1 us
    pallas_call x1, Pallas kernels, local_step(): pl.pallas_call(functools.partial(write_kernel, n), out_shape=(jax.ShapeDt...  5.49 us

profile of v2, /device:TPU:21, one launch (start us, length us, event | category | flops | bytes accessed | tf_op | source)
XLA Modules:
  0.0 65.4 jit_solution(7175367225401378484)
XLA Ops:
  0.6 0.0 copy-start
  0.6 59.1 %experts.1 = (bf16[2,1536,1024]{2,1,0:T(8,128)(2,1)S(1)}, bf16[2,1536,1024]{2,1,0:T(8,128)(2,1)S(1)}, bf16[2,1024,1024]{2,1,0:T(8,128)(2,1)S(1)}, bf16[2,512,102...) custom-call(bf16[16,2,96,1024]{3,2,1,0:T(8,128)(2,1)} %x_hbm.1, ...), custom_call_target="tpu_custom_call" | custom-call | tf_op jit(solution)/shard_map/experts/pallas_call | solution.py:358
  59.8 0.0 copy-done
  59.8 5.5 %write_out.1 = (bf16[16,2,96,1024]{3,2,1,0:T(8,128)(2,1)}, bf16[2,1024,512]{2,1,0:T(8,128)(2,1)}, bf16[2,1024,512]{2,1,0:T(8,128)(2,1)}, bf16[2,512,1024]{2,1,0:T(8,128)(2,1)}, f32[8,192]{1,0:T(8,128)}) custom-call(bf16[2,1536,1024]{2,1,0:T(8,128)(2,1)S(1)} %get-tuple-element.16.ybuf, bf16[2,1536,1024]{2,1,0:T(8,128)(2,1)S(1)} %get-tuple-element.17.xbuf, ...), custom_call_target="tpu_custom_call" | custom-call | tf_op jit(solution)/shard_map/write_out/pallas_call | solution.py:387
Async XLA Ops:
  0.6 59.1 %copy-start = (s32[192,8]{0,1:T(8,128)S(1)}, s32[192,8]{0,1:T(8,128)}, u32[]{:S(2)}) copy-start(s32[192,8]{0,1:T(8,128)} %param.14) | copy-start | bytes 18436

commit v3 on v2

--- a/solution.py
+++ b/solution.py
@@ -17,21 +17,31 @@
     return lax.dot_general(a, b, (((ca,), (cb,)), ((), ())), preferred_element_type=F32)
 
 
+def rem(a, b):
+    return a % b if isinstance(a, int) else lax.rem(a, jnp.int32(b))
+
+
+def half_of(a):
+    return a // 2 if isinstance(a, int) else lax.div(a, jnp.int32(2))
+
+
 def peers(n):
     me = lax.axis_index('ep')
     chips = n // 2
-    z, core = me // 2, me % 2
+    z, core = half_of(me), rem(me, 2)
     sgn = 1 - 2 * core
     sib = z * 2 + 1 - core
-    nxt = ((z + sgn + chips) % chips) * 2 + core
+    nxt = rem(z + sgn + chips, chips) * 2 + core
 
     def src(k):
-        p, side = k // 2, k % 2
-        dist, blk = (p + 1) // 2, (p + 1) % 2
-        chip = (z + chips - sgn * (1 - 2 * side) * dist) % chips
-        other = (side + blk) % 2
-        ring_core = jnp.where(p == 0, (core + side) % 2, (core + other) % 2)
-        return chip * 2 + ring_core
+        p, side = half_of(k), rem(k, 2)
+        dist = half_of(p + 1)
+        chip = rem(z + chips - sgn * (1 - 2 * side) * dist, chips)
+        if isinstance(p, int):
+            flip = side if p == 0 else side + p + 1
+        else:
+            flip = side + jnp.where(p == 0, 0, p + 1)
+        return chip * 2 + rem(core + flip, 2)
 
     return me, sib, nxt, src
 
@@ -58,7 +68,7 @@
 
     @pl.loop(1, n)
     def _(i):
-        pl.semaphore_signal(barrier, inc=1, device_id={'ep': (me + i) % n}, device_id_type=pl.DeviceIdType.MESH)
+        pl.semaphore_signal(barrier, inc=1, device_id={'ep': rem(me + i, n)}, device_id_type=pl.DeviceIdType.MESH)
 
     own_load = pltpu.make_async_copy(do_hbm, gbuf.at[0], g_sem)
     own_load.start()
@@ -87,26 +97,19 @@
         rt_src[e // e_loc, pl.ds(e % e_loc, 1), :] = jnp.sum(jnp.where(hit, slot1, 0.0), axis=0, keepdims=True) - 1.0
         rt_src[e // e_loc, pl.ds(e_loc + e % e_loc, 1), :] = jnp.sum(jnp.where(hit, gate, 0.0), axis=0, keepdims=True)
 
-    own_load.wait()
-    pl.semaphore_wait(barrier, n - 1)
-
     def chunk(k, m):
-        return gbuf.at[k, pl.ds(pl.multiple_of((m % 2) * half, 32), half), :]
+        return gbuf.at[k, pl.ds(pl.multiple_of(rem(m, 2) * half, 32), half), :]
 
     def ring_copy(m, k_from):
-        return remote(chunk(k_from, m), chunk(2 + 2 * (m // 2), m), ring_s.at[m], ring_r.at[m], nxt)
+        return remote(chunk(k_from, m), chunk(2 + 2 * half_of(m), m), ring_s.at[m], ring_r.at[m], nxt)
 
     def sib_copy(m):
-        k = 2 + 2 * (m // 2)
+        k = 2 + 2 * half_of(m)
         return remote(chunk(k, m), chunk(k + 1, m), sib_s.at[m], sib_r.at[m], sib)
 
     own_copy = remote(gbuf.at[0], gbuf.at[1], own_s, own_r, sib)
-    for m in range(2):
-        ring_copy(m, 0).start()
-    own_copy.start()
-
     def comm(m):
-        k = 2 + 2 * (m // 2)
+        k = 2 + 2 * half_of(m)
         ring_copy(m, k).wait_recv()
         if isinstance(m, int):
             if m + 4 < steps:
@@ -118,7 +121,7 @@
         sib_copy(m).start()
 
     def route_copy(i):
-        return remote(rt_src.at[(me + i) % n], rt_dst.at[me], rt_s.at[i], rt_r.at[i], (me + i) % n)
+        return remote(rt_src.at[rem(me + i, n)], rt_dst.at[me], rt_s.at[i], rt_r.at[i], rem(me + i, n))
 
     tile = tile_src * cap
     n_tiles = rows // tile
@@ -141,7 +144,8 @@
             ybuf[e, r, cols] = dot(ht, wd[e, :, cols], 1, 0).astype(BF16)
 
     def a_wait(i):
-        e, t = i % e_loc, i // e_loc
+        e = rem(i, e_loc)
+        t = i // e_loc if isinstance(i, int) else lax.div(i, jnp.int32(e_loc))
 
         @pl.when(e == 0)
         def _():
@@ -160,6 +164,14 @@
     for k in range(tile_src, n):
         x_load(k).start()
     phase_a(0, 0)
+
+    own_load.wait()
+    pl.semaphore_wait(barrier, n - 1)
+    for m in range(2):
+        ring_copy(m, 0).start()
+    own_copy.start()
+    a_wait(1)
+    phase_a(1, 0)
     own_copy.wait_recv()
     for m in range(2, 4):
         ring_copy(m, 1).start()
@@ -169,15 +181,14 @@
         route_copy(i).start()
     rt_dst[me] = rt_src[me]
 
-    @pl.loop(1, n_tiles * e_loc)
+    @pl.loop(2, n_tiles * e_loc)
     def _(i):
         a_wait(i)
-        phase_a(i % e_loc, i // e_loc)
-
-        @pl.when(i % 3 != 0)
+        phase_a(rem(i, e_loc), lax.div(i, jnp.int32(e_loc)))
+
+        @pl.when((i >= 4) & (i != 5))
         def _():
-            comm((2 * i - 1) // 3)
-    done_m = (2 * (n_tiles * e_loc - 1) - 1) // 3 + 1
+            comm(lax.div(2 * (i - 4), jnp.int32(3)))
 
     @pl.loop(1, n)
     def _(i):
@@ -212,7 +223,7 @@
 
     def gg_copy(k):
         s = src(k)
-        off = (s - me + n) % n
+        off = rem(s - me + n, n)
         return remote(gg_src.at[k], gg_dst.at[me], gg_s.at[off], gg_r.at[off], s)
 
     def gg_send(k0, k1):
@@ -247,57 +258,87 @@
         for c in range(dim // MXU):
             ybuf[e, r, pl.ds(c * MXU, MXU)] = dot(da, wgu[e, pl.ds(c * MXU, MXU), :], 1, 1).astype(BF16)
 
-    next_m = [done_m]
-
-    def comm_next(count=1):
-        for _ in range(count):
-            if next_m[0] < steps:
-                comm(next_m[0])
-                next_m[0] += 1
-
     kept = x_grad_rows(rows)
-    stages = [(0, 3, 0, 512), (3, 5, 512, 768), (5, 7, 768, 1280), (7, 8, 1280, 1536)]
-    for p0, p1, w0, w1 in stages:
-        need = 2 * (p1 - 1)
-        if next_m[0] < need:
-            comm_next(need - next_m[0])
-        for p in range(max(p0, 1), p1):
-            for m in (2 * p - 2, 2 * p - 1):
-                sib_copy(m).wait_recv()
-
-        for k in range(2 * p0, 2 * p1):
-            select_rows(k)
-        comm_next()
-
+
+    def sel(*ps):
+        for p in ps:
+            if p > 0:
+                for m in (2 * p - 2, 2 * p - 1):
+                    sib_copy(m).wait_recv()
+        for p in ps:
+            select_rows(2 * p)
+            select_rows(2 * p + 1)
+
+    def hid(p0, p1):
         for e in range(e_loc):
             hidden_grads(e, 2 * p0 * cap, 2 * p1 * cap)
-        gg_send(2 * p0, 2 * p1)
-        comm_next()
-
+            if e == 0:
+                gg_send(2 * p0, 2 * p1)
+
+    def wgd(w0, w1):
         @pl.loop(0, e_loc)
         def _(e):
             weight_grad(hbuf, ybuf, acc_d, wd, w0, w1, e)
-        comm_next()
-
-        if w1 <= kept:
+
+    def wgx(w0, w1, *ms):
+        if len(ms) == e_loc or not ms:
+            @pl.loop(0, e_loc)
+            def _(e):
+                weight_grad(xbuf, dab, acc_gu, xbuf, w0, w1, e)
+                if ms:
+                    comm(ms[0] + e)
+        else:
             for e in range(e_loc):
-                x_grad(e, w0, w1)
-        comm_next()
-
-        @pl.loop(0, e_loc)
-        def _(e):
-            weight_grad(xbuf, dab, acc_gu, xbuf, w0, w1, e)
-        comm_next()
+                weight_grad(xbuf, dab, acc_gu, xbuf, w0, w1, e)
+                if e < len(ms):
+                    comm(ms[e])
+
+    def gx(e, w0, w1):
+        x_grad(e, w0, w1)
+
+    sel(0, 1)
+    comm(3)
+    hid(0, 2)
+    sel(2)
+    comm(4)
+    hid(2, 3)
+    wgd(0, 512)
+    wgx(0, 512, 5, 6)
+    gx(0, 0, 512)
+    comm(7)
+    sel(3)
+    gx(1, 0, 512)
+    comm(8)
+    sel(4)
+    hid(3, 5)
+    comm(9)
+    wgd(512, 768)
+    wgx(512, 768, 10)
+    sel(5)
+    gx(0, 512, 768)
+    comm(11)
+    gx(1, 512, 768)
+    sel(6)
+    comm(12)
+    hid(5, 7)
+    wgd(768, 1280)
+    wgx(768, 1280, 13)
+    sel(7)
+    hid(7, 8)
+    wgd(1280, rows)
+
+    wgx(1280, rows)
+
+    for m in range(steps):
+        ring_copy(m, 0).wait_send()
+        sib_copy(m).wait_send()
+    own_copy.wait_send()
 
     @pl.loop(1, n)
     def _(k):
         gg_copy(k).wait_recv()
         gg_copy(k).wait_send()
         route_copy(k).wait_send()
-    for m in range(steps):
-        ring_copy(m, 0).wait_send()
-        sib_copy(m).wait_send()
-    own_copy.wait_send()
     gg_out[...] = gg_dst[...]
 
 

time: 65.5 us -> 61.7 us (0.942)
  Pallas kernels: 64.6 us -> 60.7 us
    pallas_call x1, Pallas kernels: 59.1 us -> 55.2 us  [local_step(): pl.pallas_call(functools.partial(main_kernel, n), out_shape=(pltpu.VMEM((...]
where the time goes in v3:
time: 61.7 us; the launch traced here: 61.5 us
  Pallas kernels  60.7 us (98%)
  between operations  0.84 us (1%)
    pallas_call x1, Pallas kernels, local_step(): pl.pallas_call(functools.partial(main_kernel, n), out_shape=(pltpu.VMEM((...  55.2 us
    pallas_call x1, Pallas kernels, local_step(): pl.pallas_call(functools.partial(write_kernel, n), out_shape=(jax.ShapeDt...  5.49 us

profile of v3, /device:TPU:21, one launch (start us, length us, event | category | flops | bytes accessed | tf_op | source)
XLA Modules:
  0.0 61.5 jit_solution(720685293549425041)
XLA Ops:
  0.6 0.0 copy-start
  0.6 55.2 %experts.1 = (bf16[2,1536,1024]{2,1,0:T(8,128)(2,1)S(1)}, bf16[2,1536,1024]{2,1,0:T(8,128)(2,1)S(1)}, bf16[2,1024,1024]{2,1,0:T(8,128)(2,1)S(1)}, bf16[2,512,102...) custom-call(bf16[16,2,96,1024]{3,2,1,0:T(8,128)(2,1)} %x_hbm.1, ...), custom_call_target="tpu_custom_call" | custom-call | tf_op jit(solution)/shard_map/experts/pallas_call | solution.py:399
  55.9 0.0 copy-done
  55.9 5.5 %write_out.1 = (bf16[16,2,96,1024]{3,2,1,0:T(8,128)(2,1)}, bf16[2,1024,512]{2,1,0:T(8,128)(2,1)}, bf16[2,1024,512]{2,1,0:T(8,128)(2,1)}, bf16[2,512,1024]{2,1,0:T(8,128)(2,1)}, f32[8,192]{1,0:T(8,128)}) custom-call(bf16[2,1536,1024]{2,1,0:T(8,128)(2,1)S(1)} %get-tuple-element.16.ybuf, bf16[2,1536,1024]{2,1,0:T(8,128)(2,1)S(1)} %get-tuple-element.17.xbuf, ...), custom_call_target="tpu_custom_call" | custom-call | tf_op jit(solution)/shard_map/write_out/pallas_call | solution.py:428
Async XLA Ops:
  0.6 55.2 %copy-start = (s32[192,8]{0,1:T(8,128)S(1)}, s32[192,8]{0,1:T(8,128)}, u32[]{:S(2)}) copy-start(s32[192,8]{0,1:T(8,128)} %param.14) | copy-start | bytes 18436

commit v4 on v3

--- a/solution.py
+++ b/solution.py
@@ -49,7 +49,7 @@
 def main_kernel(n, x_hbm, wg_hbm, wu_hbm, wd_hbm, do_hbm, slot_ref, eid_ref, gate_ref,
                 ybuf, xbuf, wgu, wd, dab, gg_out,
                 gbuf, pbuf, qbuf, hbuf, acc_gu, acc_d, rt_src, rt_dst, gg_src, gg_dst,
-                x_sem, w_sem, g_sem, ring_s, ring_r, sib_s, sib_r, own_s, own_r,
+                x_sem, w_sem, g_sem, ring_s, ring_r, sib_s, sib_r, own_r,
                 rt_s, rt_r, gg_s, gg_r):
     e_loc, cap, dim = x_hbm.shape[1], x_hbm.shape[2], x_hbm.shape[3]
     ffn = wd_hbm.shape[1]
@@ -101,13 +101,13 @@
         return gbuf.at[k, pl.ds(pl.multiple_of(rem(m, 2) * half, 32), half), :]
 
     def ring_copy(m, k_from):
-        return remote(chunk(k_from, m), chunk(2 + 2 * half_of(m), m), ring_s.at[m], ring_r.at[m], nxt)
+        return remote(chunk(k_from, m), chunk(2 + 2 * half_of(m), m), ring_s, ring_r.at[m], nxt)
 
     def sib_copy(m):
         k = 2 + 2 * half_of(m)
-        return remote(chunk(k, m), chunk(k + 1, m), sib_s.at[m], sib_r.at[m], sib)
-
-    own_copy = remote(gbuf.at[0], gbuf.at[1], own_s, own_r, sib)
+        return remote(chunk(k, m), chunk(k + 1, m), sib_s, sib_r.at[m], sib)
+
+    own_copy = remote(gbuf.at[0], gbuf.at[1], sib_s, own_r, sib)
     def comm(m):
         k = 2 + 2 * half_of(m)
         ring_copy(m, k).wait_recv()
@@ -121,7 +121,7 @@
         sib_copy(m).start()
 
     def route_copy(i):
-        return remote(rt_src.at[rem(me + i, n)], rt_dst.at[me], rt_s.at[i], rt_r.at[i], rem(me + i, n))
+        return remote(rt_src.at[rem(me + i, n)], rt_dst.at[me], rt_s, rt_r, rem(me + i, n))
 
     tile = tile_src * cap
     n_tiles = rows // tile
@@ -190,9 +190,9 @@
         def _():
             comm(lax.div(2 * (i - 4), jnp.int32(3)))
 
-    @pl.loop(1, n)
-    def _(i):
-        route_copy(i).wait_recv()
+    everyone = pl.ds(0, n - 1)
+    all_routes = remote(rt_src.at[everyone], rt_dst.at[everyone], rt_s, rt_r, sib)
+    all_routes.wait_recv()
 
     wide = rt_dst.shape[2]
     slot_no = lax.broadcasted_iota(jnp.int32, (cap, wide), 0).astype(F32)
@@ -223,8 +223,7 @@
 
     def gg_copy(k):
         s = src(k)
-        off = rem(s - me + n, n)
-        return remote(gg_src.at[k], gg_dst.at[me], gg_s.at[off], gg_r.at[off], s)
+        return remote(gg_src.at[k], gg_dst.at[me], gg_s, gg_r, s)
 
     def gg_send(k0, k1):
         for k in range(k0, k1):
@@ -329,16 +328,14 @@
 
     wgx(1280, rows)
 
-    for m in range(steps):
-        ring_copy(m, 0).wait_send()
-        sib_copy(m).wait_send()
-    own_copy.wait_send()
-
-    @pl.loop(1, n)
-    def _(k):
-        gg_copy(k).wait_recv()
-        gg_copy(k).wait_send()
-        route_copy(k).wait_send()
+    all_routes.wait_send()
+    blocks = pl.ds(0, steps // 2)
+    remote(gbuf.at[blocks], gbuf.at[blocks], ring_s, own_r, nxt).wait_send()
+    blocks = pl.ds(0, pairs)
+    remote(gbuf.at[blocks], gbuf.at[blocks], sib_s, own_r, sib).wait_send()
+    all_gg = remote(gg_src.at[everyone], gg_dst.at[everyone], gg_s, gg_r, sib)
+    all_gg.wait_send()
+    all_gg.wait_recv()
     gg_out[...] = gg_dst[...]
 
 
@@ -418,8 +415,8 @@
                 pltpu.VMEM((n, e_loc, wide), F32),
                 pltpu.VMEM((n, e_loc, wide), F32),
                 dma((n,)), dma((e_loc, 3)), dma,
-                dma((steps,)), dma((steps,)), dma((steps,)), dma((steps,)), dma, dma,
-                dma((n,)), dma((n,)), dma((n,)), dma((n,)),
+                dma, dma((steps,)), dma, dma((steps,)), dma,
+                dma, dma, dma, dma,
             ],
             compiler_params=pltpu.CompilerParams(collective_id=0, has_side_effects=True,
                                                  vmem_limit_bytes=39 * 1024 * 1024),

time: 61.7 us -> 60.6 us (0.982)
  Pallas kernels: 60.7 us -> 59.6 us
    pallas_call x1, Pallas kernels: 55.2 us -> 54.2 us  [local_step(): pl.pallas_call(functools.partial(main_kernel, n), out_shape=(pltpu.VMEM((...]
where the time goes in v4:
time: 60.6 us; the launch traced here: 60.5 us
  Pallas kernels  59.6 us (98%)
  between operations  0.84 us (1%)
    pallas_call x1, Pallas kernels, local_step(): pl.pallas_call(functools.partial(main_kernel, n), out_shape=(pltpu.VMEM((...  54.2 us
    pallas_call x1, Pallas kernels, local_step(): pl.pallas_call(functools.partial(write_kernel, n), out_shape=(jax.ShapeDt...  5.49 us

profile of v4, /device:TPU:21, one launch (start us, length us, event | category | flops | bytes accessed | tf_op | source)
XLA Modules:
  0.0 60.5 jit_solution(8909143798933427786)
XLA Ops:
  0.6 0.0 copy-start
  0.6 54.2 %experts.1 = (bf16[2,1536,1024]{2,1,0:T(8,128)(2,1)S(1)}, bf16[2,1536,1024]{2,1,0:T(8,128)(2,1)S(1)}, bf16[2,1024,1024]{2,1,0:T(8,128)(2,1)S(1)}, bf16[2,512,102...) custom-call(bf16[16,2,96,1024]{3,2,1,0:T(8,128)(2,1)} %x_hbm.1, ...), custom_call_target="tpu_custom_call" | custom-call | tf_op jit(solution)/shard_map/experts/pallas_call | solution.py:396
  54.8 0.0 copy-done
  54.8 5.5 %write_out.1 = (bf16[16,2,96,1024]{3,2,1,0:T(8,128)(2,1)}, bf16[2,1024,512]{2,1,0:T(8,128)(2,1)}, bf16[2,1024,512]{2,1,0:T(8,128)(2,1)}, bf16[2,512,1024]{2,1,0:T(8,128)(2,1)}, f32[8,192]{1,0:T(8,128)}) custom-call(bf16[2,1536,1024]{2,1,0:T(8,128)(2,1)S(1)} %get-tuple-element.16.ybuf, bf16[2,1536,1024]{2,1,0:T(8,128)(2,1)S(1)} %get-tuple-element.17.xbuf, ...), custom_call_target="tpu_custom_call" | custom-call | tf_op jit(solution)/shard_map/write_out/pallas_call | solution.py:425
Async XLA Ops:
  0.6 54.2 %copy-start = (s32[192,8]{0,1:T(8,128)S(1)}, s32[192,8]{0,1:T(8,128)}, u32[]{:S(2)}) copy-start(s32[192,8]{0,1:T(8,128)} %param.14) | copy-start | bytes 18436
